TPU v7x, 32 devices: a whole 2x2x4 slice. The times are simulated.
32 devices in a mesh: dp: 16 (over z, y, core), sp: 2 (over x).
Axes of the slice: x: 2, y: 2, z: 4, core: 2. Of those that a mesh axis runs over, the one named last changes fastest.
Arguments:
- hidden: bfloat16 [16, 4, 128, 3584], P('dp', None, 'sp'), may hold values from -6 to 6
- segment_ids: int32 [16, 4, 128], P('dp'), may hold values from -1 to 15, as said below
- w_query: bfloat16 [3584, 3584], P(None, 'sp'), may hold values from -0.10022297 to 0.10022297
- key_matrix: bfloat16 [3584, 512], P(None, 'sp'), may hold values from -0.10022297 to 0.10022297
- value_matrix: bfloat16 [3584, 512], P(None, 'sp'), may hold values from -0.10022297 to 0.10022297
Outputs:
- mixed: bfloat16 [16, 512, 3584], P('dp', 'sp')
Inputs may be any that keep to these rules, and one draw needn't show every extreme that they name: `segment_ids`: in each outbox the live slots come first; over them the ids start at 0 and never fall, by steps of 0 or 1; empty slots hold -1. Every group has an outbox whose 128 slots are all live.
All inputs are finite; a program needn't handle non-finite values.
Results may differ from a plain program's by a relative error of at most 0.0087.
Values may be sent and summed in bfloat16 or wider, within the bound.
No kernel may reach another device: no remote copies, remote signals or barrier semaphores. Data moves between devices by JAX's collectives and lax.ppermute only.
A program may use at most 64 MiB of HBM per device.

v0:
```python
import jax
import jax.numpy as jnp
from jax import lax
from jax.sharding import PartitionSpec as P

HEAD_SIZE = 128
NSEG = 16
GROUP_SLOTS = 512
ROPE_BASE = 1000000.0


def shifted(value, axis, steps):
    count = lax.axis_size(axis)
    pairs = [(source, (source + steps) % count) for source in range(count)]
    return lax.ppermute(value, axis, pairs)


def rotate(tensor, where):
    half_width = tensor.shape[-1] // 2
    freq = ROPE_BASE ** (-(jnp.arange(half_width, dtype=jnp.float32) * 2.0 / tensor.shape[-1]))
    angle = where[:, None] * freq[None, :]
    cosine = jnp.cos(angle)[:, None, :]
    sine = jnp.sin(angle)[:, None, :]
    first = tensor[..., :half_width]
    second = tensor[..., half_width:]
    return jnp.concatenate(
        [first * cosine - second * sine, second * cosine + first * sine], axis=-1
    )


def positions(segments):
    slot_ids = jnp.arange(NSEG, dtype=jnp.int32)
    onehot = (segments[..., :, None] == slot_ids).astype(jnp.int32)
    living = (segments >= 0).astype(jnp.int32)
    below = jnp.sum(
        (segments[..., :, None] < slot_ids).astype(jnp.int32) * living[..., :, None], axis=-2
    )
    first_slot = jnp.sum(onehot * below[..., None, :], axis=-1)
    index = jnp.arange(segments.shape[-1], dtype=jnp.int32)
    return (index - first_slot).astype(jnp.float32)


def attend(queries, projected_key_rows, projected_value_rows, labels):
    total_rows = queries.shape[0]
    kv_heads = projected_key_rows.shape[1]
    queries = queries.reshape(total_rows, kv_heads, -1, queries.shape[-1])
    scores = jnp.einsum(
        "qcgd,kcd->cgqk", queries, projected_key_rows, preferred_element_type=jnp.float32
    )
    scores = scores / jnp.sqrt(jnp.float32(queries.shape[-1]))
    index = jnp.arange(total_rows, dtype=jnp.int32)
    seen = (
        (labels[:, None] == labels[None, :])
        & (labels[:, None] >= 0)
        & (index[None, :] <= index[:, None])
    )
    seen = seen | (index[:, None] == index[None, :])
    scores = jnp.where(seen, scores, -1e30)
    largest = jnp.max(scores, axis=-1, keepdims=True)
    expo = jnp.where(seen, jnp.exp(scores - largest), 0.0)
    denominator = jnp.sum(expo, axis=-1, keepdims=True)
    probs = expo.astype(jnp.bfloat16)
    summed = jnp.einsum(
        "cgqk,kcd->qcgd", probs, projected_value_rows, preferred_element_type=jnp.float32
    )
    summed = summed / jnp.transpose(denominator, (2, 0, 1, 3))
    living = (labels >= 0).astype(jnp.float32)
    return (summed.reshape(total_rows, -1) * living[:, None]).astype(jnp.bfloat16)


def local(hidden, segment_ids, w_query, key_matrix, value_matrix):
    outboxes = hidden.shape[1]
    arrivals = [(hidden[:, 0], segment_ids[:, 0])]
    for stride in range(1, outboxes):
        arrivals.append(shifted((hidden[:, stride], segment_ids[:, stride]), "dp", stride))
    tokens_in = jnp.stack([entry[0] for entry in arrivals], axis=1)
    segments = jnp.stack([entry[1] for entry in arrivals], axis=1)
    where_all = positions(segments)
    box_ids = jnp.arange(outboxes, dtype=jnp.int32)[None, :, None]
    labels = jnp.where(segments >= 0, box_ids * NSEG + segments, -1).reshape(-1)
    query_cols = w_query.shape[1]
    key_cols = key_matrix.shape[1]
    w_joined = jnp.concatenate([w_query, key_matrix, value_matrix], axis=1)
    portion = lax.all_gather(tokens_in, "sp", axis=2, tiled=True)
    width_rows = portion.shape[2]
    flat = portion.reshape(-1, portion.shape[3])
    product = jnp.dot(flat, w_joined, preferred_element_type=jnp.float32)
    where_part = where_all.reshape(-1)
    queries = rotate(
        product[:, :query_cols].reshape(flat.shape[0], -1, HEAD_SIZE), where_part
    ).astype(jnp.bfloat16)
    projected_key_rows = rotate(
        product[:, query_cols : query_cols + key_cols].reshape(flat.shape[0], -1, HEAD_SIZE),
        where_part,
    ).astype(jnp.bfloat16)
    projected_value_rows = product[:, query_cols + key_cols :].astype(jnp.bfloat16)
    joined = jnp.concatenate(
        [
            queries.reshape(flat.shape[0], -1),
            projected_key_rows.reshape(flat.shape[0], -1),
            projected_value_rows,
        ],
        axis=1,
    )
    projected = joined.reshape(1, outboxes, width_rows, -1)
    projected = projected.reshape(GROUP_SLOTS, -1)
    queries = projected[:, :query_cols].reshape(GROUP_SLOTS, -1, HEAD_SIZE)
    projected_key_rows = projected[:, query_cols : query_cols + key_cols].reshape(
        GROUP_SLOTS, -1, HEAD_SIZE
    )
    projected_value_rows = projected[:, query_cols + key_cols :].reshape(GROUP_SLOTS, -1, HEAD_SIZE)
    attended = attend(queries, projected_key_rows, projected_value_rows, labels).reshape(
        1, GROUP_SLOTS, -1
    )
    return lax.all_to_all(attended, "sp", split_axis=1, concat_axis=2, tiled=True)


def solution(mesh):
    placed = (
        P("dp", None, "sp", None),
        P("dp", None, None),
        P(None, "sp"),
        P(None, "sp"),
        P(None, "sp"),
    )
    return jax.shard_map(
        local, mesh=mesh, in_specs=placed, out_specs=P("dp", "sp", None), check_vma=False
    )
```

profile of v0, /device:TPU:0, one launch (start us, length us, event | category | flops | bytes accessed | tf_op | source)
XLA Modules:
  0.0 220.1 jit_solution(8252332415008291170)
XLA Ops:
  6.5 1.6 fusion.32
  8.1 2.5 %collective-permute-start.2 = (bf16[1,64,3584]{2,1,0:T(8,128)(2,1)S(1)}, bf16[1,64,3584]{2,1,0:T(8,128)(2,1)S(1)}, u32[]{:S(2)}, u32[]{:S(2)}) collective-permute-start(bf16[1,64,3584]{2,1,0:T(8,128)(2,1)S(1)} %get-tuple-element.12), channel_id=1, source_target_pairs={{0,6},{2,8},{4,10},{6,12},{8,14},{10,16},{12,18},{14,20},{16,22},{... | collective-permute-start | bytes 1376264 | tf_op jit(solution)/shard_map/ppermute | solution.py:15
  10.6 1.5 collective-permute-start.1
  12.6 7.7 %collective-permute-done.2 = bf16[1,64,3584]{2,1,0:T(8,128)(2,1)S(1)} collective-permute-done((bf16[1,64,3584]{2,1,0:T(8,128)(2,1)S(1)}, bf16[1,64,3584]{2,1,0:T(8,128)(2,1)S(1)}, u32[]{:S(2)}, u32[]{:S(2)}) %collective-permute-start.2) | collective-permute-done | bytes 458784 | tf_op jit(solution)/shard_map/ppermute | solution.py:15
  20.2 15.2 %collective-permute-done.1 = bf16[1,64,3584]{2,1,0:T(8,128)(2,1)S(1)} collective-permute-done((bf16[1,64,3584]{2,1,0:T(8,128)(2,1)S(1)}, bf16[1,64,3584]{2,1,0:T(8,128)(2,1)S(1)}, u32[]{:S(2)}, u32[]{:S(2)}) %collective-permute-start.1) | collective-permute-done | bytes 458784 | tf_op jit(solution)/shard_map/ppermute | solution.py:15
  35.4 4.6 %collective-permute-done = bf16[1,64,3584]{2,1,0:T(8,128)(2,1)S(1)} collective-permute-done((bf16[1,64,3584]{2,1,0:T(8,128)(2,1)S(1)}, bf16[1,64,3584]{2,1,0:T(8,128)(2,1)S(1)}, u32[]{:S(2)}, u32[]{:S(2)}) %collective-permute-start) | collective-permute-done | bytes 458784 | tf_op jit(solution)/shard_map/ppermute | solution.py:15
  40.0 1.5 pad_maximum_fusion
  41.7 4.6 %collective-permute-done.5 = s32[1,128]{1,0:T(1,128)S(1)} collective-permute-done((s32[1,128]{1,0:T(1,128)S(1)}, s32[1,128]{1,0:T(1,128)S(1)}, u32[]{:S(2)}, u32[]{:S(2)}) %collective-permute-start.5) | collective-permute-done | bytes 544 | tf_op jit(solution)/shard_map/ppermute | solution.py:15
  46.3 1.5 collective-permute-done.4
  49.0 1.0 fusion.20
  50.0 40.8 %all-gather.2.cloned.1.call-done = bf16[1,4,128,3584]{3,2,1,0:T(8,128)(2,1)} async-done(((bf16[1,4,64,3584]{3,2,1,0:T(8,128)(2,1)}), bf16[1,4,128,3584]{3,2,1,0:T(8,128)(2,1)}) %all-gather.2.cloned.1.call-update) | async-done | bytes 3670032 | tf_op jit(solution)/shard_map/all_gather | solution.py:84
  90.9 13.2 %fusion.1 = f32[512,2304]{1,0:T(8,128)S(1)} fusion(bf16[512,3584]{1,0:T(8,128)(2,1)} %bitcast.96, bf16[3584,256]{1,0:T(8,128)(2,1)S(1)} %copy-done.5, bf16[3584,256]{1,0:T(8,128)(2,1)} %param.8, bf16[3584,1792]{1,0:T(8,128)(2,1)} %param.7), kind=kOutput, calls=%fused_computation.1 | convolution fusion | flops 8505262080 | bytes 24903680 | tf_op jit(solution)/shard_map/dot_general | solution.py:87
  104.1 2.2 %slice.65 = f32[512,1792]{1,0:T(8,128)} slice(f32[512,2304]{1,0:T(8,128)S(1)} %fusion.1), slice={[0:512], [0:1792]} | slice | bytes 7340032 | tf_op jit(solution)/shard_map/slice | solution.py:90
  106.3 1.0 copy-done.1
  107.3 0.8 copy.97
  108.1 5.1 %copy.85 = f32[512,1792]{0,1:T(8,128)} copy(f32[512,1792]{1,0:T(8,128)} %slice.65) | data formatting | bytes 7340032 | tf_op jit(solution)/shard_map/slice | solution.py:90
  113.2 3.9 %subtract_convert_fusion = (bf16[512,14,64]{0,2,1:T(8,128)(2,1)}, bf16[512,14,64]{0,2,1:T(8,128)(2,1)}) fusion(f32[512,14,128]{0,2,1:T(8,128)} %bitcast.77, f32[512,64]{0,1:T(8,128)S(1)} %get-tuple-element.19, f32[512,64]{0,1:T(8,128)S(1)} %get-tuple-element.18), kind=kLoop, calls=%fused_computation.23 | loop fusion | flops 3670016 | bytes 5767168 | tf_op jit(solution)/shard_map/convert.3
  117.1 2.0 copy.87
  119.1 2.6 %copy.86 = bf16[512,14,64]{2,0,1:T(8,128)(2,1)} copy(bf16[512,14,64]{0,2,1:T(8,128)(2,1)} %get-tuple-element.8) | data formatting | bytes 1835008 | tf_op jit(solution)/shard_map/convert.3
  123.5 7.4 %fusion.15 = f32[2,512,512,7]{2,1,3,0:T(8,128)} fusion(bf16[512,2,7,64]{3,0,2,1:T(8,128)(2,1)S(1)} %bitcast.80, bf16[512,2,7,64]{3,0,2,1:T(8,128)(2,1)S(1)} %bitcast.81, bf16[512,2,64]{2,0,1:T(8,128)(2,1)S(1)} %get-tuple-element.15, bf16[512,2,64]{2,0,1:T(8,128)(2,1)S(1)} %get-tuple-element.14), kind=kOutput, calls=%fused_computation.18 | convolution fusion | flops 943718400 | bytes 16777216 | tf_op jit(solution)/shard_map/qcgd,kcd->cgqk/dot_general | solution.py:47
  130.8 13.6 %fusion.35 = (f32[2,7,512]{2,1,0:T(8,128)S(1)}, bf16[2,7,512,512]{2,3,1,0:T(8,128)(2,1)S(1)}) fusion(f32[2,512,512,7]{2,1,3,0:T(8,128)} %fusion.15, pred[512,512]{0,1:T(8,128)(4,1)S(1)} %copy-done.2), kind=kOutput, calls=%fused_computation.66 | output fusion | flops 29360640 | bytes 22310912 | tf_op jit(solution)/shard_map/sub | solution.py:60
  144.5 2.9 %bitcast_divide_fusion = f32[512,2,7,128]{0,3,2,1:T(8,128)} fusion(bf16[512,2,128,1]{0,2,3,1:T(8,128)(2,1)S(1)} %bitcast.88, bf16[2,7,512,512]{2,3,1,0:T(8,128)(2,1)S(1)} %get-tuple-element.26, f32[512,2,7]{0,2,1:T(8,128)S(1)} %bitcast.97), kind=kOutput, calls=%fused_computation.15 | convolution fusion | flops 940441600 | bytes 11300864 | tf_op jit(solution)/shard_map/cgqk,kcd->qcgd/dot_general | solution.py:63
  147.5 5.1 %copy.90 = f32[1,512,1792]{2,1,0:T(8,128)} copy(f32[1,512,1792]{1,2,0:T(8,128)} %bitcast.84) | data formatting | bytes 7340032 | tf_op jit(solution)/shard_map/reshape | solution.py:68
  152.6 2.3 %multiply_convert_fusion = bf16[1,512,1792]{2,1,0:T(8,128)(2,1)S(1)} fusion(f32[1,512,1792]{2,1,0:T(8,128)} %copy.90, f32[512]{0:T(512)S(1)} %get-tuple-element.5), kind=kLoop, calls=%fused_computation.16 | loop fusion | flops 1835008 | bytes 5507072 | tf_op jit(solution)/shard_map/convert_element_type | solution.py:68
  154.9 4.6 %copy.106 = bf16[1,512,1792]{2,0,1:T(2,128)(2,1)} copy(bf16[1,512,1792]{2,1,0:T(8,128)(2,1)S(1)} %multiply_convert_fusion) | data formatting | bytes 3670016 | tf_op jit(solution)/shard_map/convert_element_type | solution.py:68
  160.0 13.1 %reduce.2 = bf16[512,1792]{1,0:T(8,128)(2,1)} reduce(bf16[512,1,1792]{2,1,0:T(2,128)(2,1)} %bitcast.78, bf16[]{:T(256)} %broadcast.216), dimensions={1}, to_apply=%bitcast.76.reduce_sub_computation | reduce | bytes 3670018
  173.1 1.7 reshape.315
  174.8 25.5 %all_to_all.18 = bf16[2,2,229376]{2,1,0:T(2,128)(2,1)} all-to-all(bf16[2,2,229376]{2,1,0:T(2,128)(2,1)S(1)} %reshape.315), channel_id=1, replica_groups=mesh['dp'=16,'sp'=2] {'sp'}, dimensions={0} | all-to-all | bytes 3670016 | tf_op jit(solution)/shard_map/all_to_all | solution.py:115
  200.3 4.0 %reshape.316 = bf16[512,1,1792]{2,1,0:T(2,128)(2,1)} reshape(bf16[2,2,229376]{2,1,0:T(2,128)(2,1)} %all_to_all.18) | data formatting | bytes 3670016
  204.3 3.5 %copy.98 = bf16[1,512,1792]{2,1,0:T(8,128)(2,1)} copy(bf16[1,512,1792]{2,0,1:T(2,128)(2,1)} %bitcast.79) | data formatting | bytes 3670016
  207.8 2.8 %copy.92 = bf16[1,256,2,1792]{1,3,2,0:T(8,128)(2,1)S(1)} copy(bf16[1,256,2,1792]{3,1,2,0:T(8,128)(2,1)} %bitcast.83) | data formatting | bytes 3670016 | tf_op jit(solution)/shard_map/all_to_all | solution.py:115
  210.6 2.6 %copy.93 = bf16[1,256,3584]{2,1,0:T(8,128)(2,1)} copy(bf16[1,256,3584]{1,2,0:T(8,128)(2,1)S(1)} %bitcast.82) | data formatting | bytes 3670016 | tf_op jit(solution)/shard_map/all_to_all | solution.py:115
  (38 shorter events, 4.1 us)
Async XLA Ops:
  6.5 84.3 %all-gather.2.cloned.1.call-start = ((), (), s32[]{:S(2)}) async-start(), calls=%async_computation.1 | async-start | bytes 5505024 | tf_op jit(solution)/shard_map/all_gather | solution.py:84
  8.1 33.4 %copy-start.4 = (s32[1,4,128]{2,1,0:T(4,128)S(1)}, s32[1,4,128]{2,1,0:T(4,128)}, u32[]{:S(2)}) copy-start(s32[1,4,128]{2,1,0:T(4,128)} %param.6) | copy-start | bytes 6148
  8.1 82.8 %copy-start.5 = (bf16[3584,256]{1,0:T(8,128)(2,1)S(1)}, bf16[3584,256]{1,0:T(8,128)(2,1)}, u32[]{:S(2)}) copy-start(bf16[3584,256]{1,0:T(8,128)(2,1)} %param.9) | copy-start | bytes 5505028
  8.1 12.1 %collective-permute-start.2 = (bf16[1,64,3584]{2,1,0:T(8,128)(2,1)S(1)}, bf16[1,64,3584]{2,1,0:T(8,128)(2,1)S(1)}, u32[]{:S(2)}, u32[]{:S(2)}) collective-permute-start(bf16[1,64,3584]{2,1,0:T(8,128)(2,1)S(1)} %get-tuple-element.12), channel_id=1, source_target_pairs={{0,6},{2,8},{4,10},{6,12},{8,14},{10,16},{12,18},{14,20},{16,22},{... | collective-permute-start | bytes 1376264 | tf_op jit(solution)/shard_map/ppermute | solution.py:15
  10.6 24.8 %collective-permute-start.1 = (bf16[1,64,3584]{2,1,0:T(8,128)(2,1)S(1)}, bf16[1,64,3584]{2,1,0:T(8,128)(2,1)S(1)}, u32[]{:S(2)}, u32[]{:S(2)}) collective-permute-start(bf16[1,64,3584]{2,1,0:T(8,128)(2,1)S(1)} %get-tuple-element.13), channel_id=1, source_target_pairs={{0,4},{2,6},{4,8},{6,10},{8,12},{10,14},{12,16},{14,18},{16,20},{1... | collective-permute-start | bytes 1376264 | tf_op jit(solution)/shard_map/ppermute | solution.py:15
  12.1 27.8 %collective-permute-start = (bf16[1,64,3584]{2,1,0:T(8,128)(2,1)S(1)}, bf16[1,64,3584]{2,1,0:T(8,128)(2,1)S(1)}, u32[]{:S(2)}, u32[]{:S(2)}) collective-permute-start(bf16[1,64,3584]{2,1,0:T(8,128)(2,1)S(1)} %get-tuple-element.11), channel_id=1, source_target_pairs={{0,2},{2,4},{4,6},{6,8},{8,10},{10,12},{12,14},{14,16},{16,18},{18... | collective-permute-start | bytes 1376264 | tf_op jit(solution)/shard_map/ppermute | solution.py:15
  41.5 4.8 %collective-permute-start.5 = (s32[1,128]{1,0:T(1,128)S(1)}, s32[1,128]{1,0:T(1,128)S(1)}, u32[]{:S(2)}, u32[]{:S(2)}) collective-permute-start(s32[1,128]{1,0:T(1,128)S(1)} %get-tuple-element.23), channel_id=1, source_target_pairs={{0,6},{2,8},{4,10},{6,12},{8,14},{10,16},{12,18},{14,20},{16,22},{... | collective-permute-start | bytes 1544 | tf_op jit(solution)/shard_map/ppermute | solution.py:15
  41.5 6.3 %collective-permute-start.4 = (s32[1,128]{1,0:T(1,128)S(1)}, s32[1,128]{1,0:T(1,128)S(1)}, u32[]{:S(2)}, u32[]{:S(2)}) collective-permute-start(s32[1,128]{1,0:T(1,128)S(1)} %get-tuple-element.24), channel_id=1, source_target_pairs={{0,4},{2,6},{4,8},{6,10},{8,12},{10,14},{12,16},{14,18},{16,20},{1... | collective-permute-start | bytes 1544 | tf_op jit(solution)/shard_map/ppermute | solution.py:15
  41.6 6.3 %collective-permute-start.3 = (s32[1,128]{1,0:T(1,128)S(1)}, s32[1,128]{1,0:T(1,128)S(1)}, u32[]{:S(2)}, u32[]{:S(2)}) collective-permute-start(s32[1,128]{1,0:T(1,128)S(1)} %get-tuple-element.22), channel_id=1, source_target_pairs={{0,2},{2,4},{4,6},{6,8},{8,10},{10,12},{12,14},{14,16},{16,18},{18... | collective-permute-start | bytes 1544 | tf_op jit(solution)/shard_map/ppermute | solution.py:15
  104.1 3.2 %copy-start.1 = (f32[512,2304]{1,0:T(8,128)}, f32[512,2304]{1,0:T(8,128)S(1)}, u32[]{:S(2)}) copy-start(f32[512,2304]{1,0:T(8,128)S(1)} %fusion.1) | copy-start | bytes 14155780
  117.1 4.5 %slice-start = ((f32[512,2304]{1,0:T(8,128)}), f32[512,256]{1,0:T(8,128)S(1)}, s32[]{:S(2)}) async-start(f32[512,2304]{1,0:T(8,128)} %copy-done.1), calls=%async_computation.2 | async-start | bytes 1048576 | tf_op jit(solution)/shard_map/slice | solution.py:93
  122.0 1.5 copy-start
  123.5 7.4 %copy-start.2 = (pred[512,512]{0,1:T(8,128)(4,1)S(1)}, pred[512,512]{0,1:T(8,128)(4,1)}, u32[]{:S(2)}) copy-start(pred[512,512]{0,1:T(8,128)(4,1)} %fusion.20) | copy-start | bytes 786436
  130.8 13.7 %copy-start.3 = (bf16[512,256]{0,1:T(8,128)(2,1)S(1)}, bf16[512,256]{0,1:T(8,128)(2,1)}, u32[]{:S(2)}) copy-start(bf16[512,256]{0,1:T(8,128)(2,1)} %copy.97) | copy-start | bytes 786436
Sparse Core Ops, SparseCore 0:
  41.6 49.2 all-gather.1
where the time goes:
time: 221 us; the launch traced here: 220 us
  waiting for transfers between devices  74.4 us (34%)
  local copies, waits for them, and re-layouts  42.1 us (19%)
  other arithmetic  36.4 us (16%)
  blocking collectives  25.5 us (12%)
  matrix products  23.5 us (11%)
  between operations  13.6 us (6%)
  starting transfers between devices  4.64 us (2%)
    all_gather x1, waiting for transfers between devices, local(): portion = lax.all_gather(tokens_in, 'sp', axis=2, tiled=True)  40.8 us
    ppermute x6, waiting for transfers between devices, shifted(): return lax.ppermute(value, axis, pairs)  33.5 us
    all_to_all x1, blocking collectives, local(): lax.all_to_all(attended, 'sp', split_axis=1, concat_axis=2, tiled=True)  25.5 us
    sub x1, other arithmetic, attend(): expo = jnp.where(seen, jnp.exp(scores - largest), 0.0)  13.6 us
    dot_general x1, matrix products, local(): product = jnp.dot(flat, w_joined, preferred_element_type=jnp.float32)  13.2 us
    unnamed x1, other arithmetic  13.1 us
    unnamed x16, local copies, waits for them, and re-layouts  11.4 us
    dot_general x1, matrix products, attend(): jnp.einsum('qcgd,kcd->cgqk', queries, projected_key_rows, preferred_eleme...  7.37 us
  transfers between devices with their start and end apart: 7, of which 6 were waited for; matrix products, arithmetic and copies ran while one was open for 1% of the time, Pallas kernels for 0%

commit v1 on v0

--- a/solution.py
+++ b/solution.py
@@ -112,7 +112,10 @@
     attended = attend(queries, projected_key_rows, projected_value_rows, labels).reshape(
         1, GROUP_SLOTS, -1
     )
-    return lax.all_to_all(attended, "sp", split_axis=1, concat_axis=2, tiled=True)
+    return jnp.concatenate(
+        lax.all_to_all(jnp.stack(jnp.split(attended, lax.axis_size("sp"), axis=1)), "sp", 0, 0),
+        axis=2,
+    )
 
 
 def solution(mesh):

time: 221 us -> 181 us (0.82)
  local copies, waits for them, and re-layouts: 42.1 us -> 18.6 us
  other arithmetic: 36.4 us -> 22.5 us
  waiting for transfers between devices: 74.4 us -> 68.1 us
  starting transfers between devices: 4.64 us -> 9.7 us
    unnamed x1 -> x0, other arithmetic: 13.1 us -> none
    unnamed x16 -> x8, local copies, waits for them, and re-layouts: 11.4 us -> 0.02 us
    ppermute x6, waiting for transfers between devices: 33.5 us -> 27.8 us  [shifted(): return lax.ppermute(value, axis, pairs)]
    all_to_all x2 -> x0, local copies, waits for them, and re-layouts: 5.36 us -> none  [local(): lax.all_to_all(attended, 'sp', split_axis=1, concat_axis=2, tiled=True)]
    ppermute x6, starting transfers between devices: 4.63 us -> 9.7 us  [shifted(): return lax.ppermute(value, axis, pairs)]
    convert_element_type x1 -> x0, local copies, waits for them, and re-layouts: 4.64 us -> none  [attend(): (summed.reshape(total_rows, -1) * living[:, None]).astype(jnp.bfloat16)]
    reshape x1, local copies, waits for them, and re-layouts: 5.12 us -> 2.55 us  [local(): jnp.concatenate(lax.all_to_all(jnp.stack(jnp.split(attended, lax.axis_siz...]
    another operation x2 -> x3, other arithmetic: 4.03 us -> 5 us
  transfers between devices with their start and end apart: 7 -> 7, of which waited for: 6 -> 7; matrix products, arithmetic and copies ran while one was open for 1% -> 2% of each run, Pallas kernels for 0% -> 0%
where the time goes in v1:
time: 181 us; the launch traced here: 180 us
  waiting for transfers between devices  68.1 us (38%)
  blocking collectives  24.7 us (14%)
  matrix products  23.2 us (13%)
  other arithmetic  22.5 us (12%)
  local copies, waits for them, and re-layouts  18.6 us (10%)
  between operations  13.6 us (8%)
  starting transfers between devices  9.7 us (5%)
    all_gather x1, waiting for transfers between devices, local(): portion = lax.all_gather(tokens_in, 'sp', axis=2, tiled=True)  40.4 us
    ppermute x6, waiting for transfers between devices, shifted(): return lax.ppermute(value, axis, pairs)  27.8 us
    all_to_all x1, blocking collectives, local(): lax.all_to_all(jnp.stack(jnp.split(attended, lax.axis_size('sp'), axis=1)...  24.7 us
    sub x1, other arithmetic, attend(): expo = jnp.where(seen, jnp.exp(scores - largest), 0.0)  13.6 us
    dot_general x1, matrix products, local(): product = jnp.dot(flat, w_joined, preferred_element_type=jnp.float32)  13.2 us
    ppermute x6, starting transfers between devices, shifted(): return lax.ppermute(value, axis, pairs)  9.7 us
    dot_general x1, matrix products, attend(): jnp.einsum('qcgd,kcd->cgqk', queries, projected_key_rows, preferred_eleme...  8.9 us
    slice x2, local copies, waits for them, and re-layouts, local(): product[:, :query_cols].reshape(flat.shape[0], -1, HEAD_SIZE)  7.18 us
  transfers between devices with their start and end apart: 7, of which 7 were waited for; matrix products, arithmetic and copies ran while one was open for 2% of the time, Pallas kernels for 0%

profile of v1, /device:TPU:0, one launch (start us, length us, event | category | flops | bytes accessed | tf_op | source)
XLA Modules:
  0.0 180.3 jit_solution(2797308720457104253)
XLA Ops:
  6.5 1.6 fusion.32
  8.1 0.5 collective-permute-start
  8.7 3.7 %collective-permute-start.2 = (bf16[1,64,3584]{2,1,0:T(8,128)(2,1)S(1)}, bf16[1,64,3584]{2,1,0:T(8,128)(2,1)S(1)}, u32[]{:S(2)}, u32[]{:S(2)}) collective-permute-start(bf16[1,64,3584]{2,1,0:T(8,128)(2,1)S(1)} %get-tuple-element.14), channel_id=1, source_target_pairs={{0,6},{2,8},{4,10},{6,12},{8,14},{10,16},{12,18},{14,20},{16,22},{... | collective-permute-start | bytes 1376264 | tf_op jit(solution)/shard_map/ppermute | solution.py:15
  12.4 1.5 collective-permute-start.1
  13.9 8.5 %collective-permute-done = bf16[1,64,3584]{2,1,0:T(8,128)(2,1)S(1)} collective-permute-done((bf16[1,64,3584]{2,1,0:T(8,128)(2,1)S(1)}, bf16[1,64,3584]{2,1,0:T(8,128)(2,1)S(1)}, u32[]{:S(2)}, u32[]{:S(2)}) %collective-permute-start) | collective-permute-done | bytes 458784 | tf_op jit(solution)/shard_map/ppermute | solution.py:15
  22.5 0.8 collective-permute-done.2
  23.3 13.5 %collective-permute-done.1 = bf16[1,64,3584]{2,1,0:T(8,128)(2,1)S(1)} collective-permute-done((bf16[1,64,3584]{2,1,0:T(8,128)(2,1)S(1)}, bf16[1,64,3584]{2,1,0:T(8,128)(2,1)S(1)}, u32[]{:S(2)}, u32[]{:S(2)}) %collective-permute-start.1) | collective-permute-done | bytes 458784 | tf_op jit(solution)/shard_map/ppermute | solution.py:15
  36.8 1.5 pad_maximum_fusion
  38.3 2.5 %collective-permute-start.3 = (s32[1,128]{1,0:T(1,128)S(1)}, s32[1,128]{1,0:T(1,128)S(1)}, u32[]{:S(2)}, u32[]{:S(2)}) collective-permute-start(s32[1,128]{1,0:T(1,128)S(1)} %get-tuple-element.24), channel_id=1, source_target_pairs={{0,2},{2,4},{4,6},{6,8},{8,10},{10,12},{12,14},{14,16},{16,18},{18... | collective-permute-start | bytes 1544 | tf_op jit(solution)/shard_map/ppermute | solution.py:15
  40.9 1.3 collective-permute-start.4
  42.2 1.8 %collective-permute-done.3 = s32[1,128]{1,0:T(1,128)S(1)} collective-permute-done((s32[1,128]{1,0:T(1,128)S(1)}, s32[1,128]{1,0:T(1,128)S(1)}, u32[]{:S(2)}, u32[]{:S(2)}) %collective-permute-start.3) | collective-permute-done | bytes 544 | tf_op jit(solution)/shard_map/ppermute | solution.py:15
  44.1 1.6 collective-permute-done.5
  45.6 1.5 collective-permute-done.4
  47.4 0.5 multiply_cosine_fusion
  48.1 0.8 copy.36
  49.0 1.0 fusion.20
  50.0 40.4 %all-gather.2.cloned.1.call-done = bf16[1,4,128,3584]{3,2,1,0:T(8,128)(2,1)} async-done(((bf16[1,4,64,3584]{3,2,1,0:T(8,128)(2,1)}), bf16[1,4,128,3584]{3,2,1,0:T(8,128)(2,1)}) %all-gather.2.cloned.1.call-update) | async-done | bytes 3670032 | tf_op jit(solution)/shard_map/all_gather | solution.py:84
  90.3 13.2 %fusion.1 = f32[512,2304]{1,0:T(8,128)S(1)} fusion(bf16[512,3584]{1,0:T(8,128)(2,1)} %bitcast.92, bf16[3584,256]{1,0:T(8,128)(2,1)S(1)} %copy-done.3, bf16[3584,256]{1,0:T(8,128)(2,1)} %param.8, bf16[3584,1792]{1,0:T(8,128)(2,1)} %param.7), kind=kOutput, calls=%fused_computation.1 | convolution fusion | flops 8505262080 | bytes 24903680 | tf_op jit(solution)/shard_map/dot_general | solution.py:87
  103.6 2.0 %slice.65 = f32[512,1792]{1,0:T(8,128)} slice(f32[512,2304]{1,0:T(8,128)S(1)} %fusion.1), slice={[0:512], [0:1792]} | slice | bytes 7340032 | tf_op jit(solution)/shard_map/slice | solution.py:90
  105.6 0.8 copy.46
  106.5 5.1 %copy.37 = f32[512,1792]{0,1:T(8,128)} copy(f32[512,1792]{1,0:T(8,128)} %slice.65) | data formatting | bytes 7340032 | tf_op jit(solution)/shard_map/slice | solution.py:90
  111.6 3.6 %subtract_convert_fusion = (bf16[512,14,64]{0,2,1:T(8,128)(2,1)}, bf16[512,14,64]{0,2,1:T(8,128)(2,1)S(1)}) fusion(f32[512,14,128]{0,2,1:T(8,128)} %bitcast.76, f32[512,64]{0,1:T(8,128)S(1)} %get-tuple-element.21, f32[512,64]{0,1:T(8,128)S(1)} %get-tuple-element.20), kind=kLoop, calls=%fused_computation.24 | loop fusion | flops 3670016 | bytes 5767168 | tf_op jit(solution)/shard_map/convert.3
  115.5 1.4 fusion.33
  116.9 1.9 %copy.38 = bf16[512,14,64]{2,0,1:T(8,128)(2,1)S(1)} copy(bf16[512,14,64]{0,2,1:T(8,128)(2,1)} %get-tuple-element.8) | data formatting | bytes 1835008 | tf_op jit(solution)/shard_map/convert.3
  118.8 1.6 copy.39
  120.4 1.2 subtract_convert_fusion.1
  121.7 8.9 %fusion.15 = f32[2,512,512,7]{2,1,3,0:T(8,128)} fusion(bf16[512,2,7,64]{3,0,2,1:T(8,128)(2,1)} %bitcast.78, bf16[512,2,7,64]{3,0,2,1:T(8,128)(2,1)S(1)} %bitcast.77, bf16[512,2,64]{2,0,1:T(8,128)(2,1)S(1)} %get-tuple-element.17, bf16[512,2,64]{2,0,1:T(8,128)(2,1)S(1)} %get-tuple-element.16), kind=kOutput, calls=%fused_computation.18 | convolution fusion | flops 943718400 | bytes 16777216 | tf_op jit(solution)/shard_map/qcgd,kcd->cgqk/dot_general | solution.py:47
  130.6 13.6 %fusion.35 = (f32[2,7,512]{2,1,0:T(8,128)S(1)}, bf16[2,7,512,512]{2,3,1,0:T(8,128)(2,1)S(1)}) fusion(f32[2,512,512,7]{2,1,3,0:T(8,128)} %fusion.15, pred[512,512]{0,1:T(8,128)(4,1)S(1)} %copy-done), kind=kOutput, calls=%fused_computation.69 | output fusion | flops 29360640 | bytes 22310912 | tf_op jit(solution)/shard_map/sub | solution.py:60
  144.3 1.1 bitcast_divide_fusion
  145.4 0.5 multiply_convert_fusion
  146.3 24.7 %all_to_all.5 = bf16[2,1,256,1792]{2,3,1,0:T(8,128)(2,1)S(1)} all-to-all(bf16[2,1,256,1792]{2,3,1,0:T(8,128)(2,1)S(1)} %pad_maximum_fusion.1), channel_id=1, replica_groups=mesh['dp'=16,'sp'=2] {'sp'}, dimensions={0} | all-to-all | bytes 3670016 | tf_op jit(solution)/shard_map/all_to_all | solution.py:116
  170.9 2.5 %copy.47 = bf16[1,256,3584]{2,1,0:T(8,128)(2,1)} copy(bf16[1,256,3584]{1,2,0:T(8,128)(2,1)S(1)} %bitcast.79) | data formatting | bytes 3670016 | tf_op jit(solution)/shard_map/reshape | solution.py:115
  (27 shorter events, 1.2 us)
Async XLA Ops:
  6.5 83.8 %all-gather.2.cloned.1.call-start = ((), (), s32[]{:S(2)}) async-start(), calls=%async_computation.1 | async-start | bytes 5505024 | tf_op jit(solution)/shard_map/all_gather | solution.py:84
  8.1 30.2 %copy-start.2 = (s32[1,4,128]{2,1,0:T(4,128)S(1)}, s32[1,4,128]{2,1,0:T(4,128)}, u32[]{:S(2)}) copy-start(s32[1,4,128]{2,1,0:T(4,128)} %param.6) | copy-start | bytes 6148
  8.1 82.2 %copy-start.3 = (bf16[3584,256]{1,0:T(8,128)(2,1)S(1)}, bf16[3584,256]{1,0:T(8,128)(2,1)}, u32[]{:S(2)}) copy-start(bf16[3584,256]{1,0:T(8,128)(2,1)} %param.9) | copy-start | bytes 5505028
  8.1 14.3 %collective-permute-start = (bf16[1,64,3584]{2,1,0:T(8,128)(2,1)S(1)}, bf16[1,64,3584]{2,1,0:T(8,128)(2,1)S(1)}, u32[]{:S(2)}, u32[]{:S(2)}) collective-permute-start(bf16[1,64,3584]{2,1,0:T(8,128)(2,1)S(1)} %get-tuple-element.13), channel_id=1, source_target_pairs={{0,2},{2,4},{4,6},{6,8},{8,10},{10,12},{12,14},{14,16},{16,18},{18... | collective-permute-start | bytes 1376264 | tf_op jit(solution)/shard_map/ppermute | solution.py:15
  8.7 14.7 %collective-permute-start.2 = (bf16[1,64,3584]{2,1,0:T(8,128)(2,1)S(1)}, bf16[1,64,3584]{2,1,0:T(8,128)(2,1)S(1)}, u32[]{:S(2)}, u32[]{:S(2)}) collective-permute-start(bf16[1,64,3584]{2,1,0:T(8,128)(2,1)S(1)} %get-tuple-element.14), channel_id=1, source_target_pairs={{0,6},{2,8},{4,10},{6,12},{8,14},{10,16},{12,18},{14,20},{16,22},{... | collective-permute-start | bytes 1376264 | tf_op jit(solution)/shard_map/ppermute | solution.py:15
  12.4 24.4 %collective-permute-start.1 = (bf16[1,64,3584]{2,1,0:T(8,128)(2,1)S(1)}, bf16[1,64,3584]{2,1,0:T(8,128)(2,1)S(1)}, u32[]{:S(2)}, u32[]{:S(2)}) collective-permute-start(bf16[1,64,3584]{2,1,0:T(8,128)(2,1)S(1)} %get-tuple-element.15), channel_id=1, source_target_pairs={{0,4},{2,6},{4,8},{6,10},{8,12},{10,14},{12,16},{14,18},{16,20},{1... | collective-permute-start | bytes 1376264 | tf_op jit(solution)/shard_map/ppermute | solution.py:15
  38.3 5.7 %collective-permute-start.3 = (s32[1,128]{1,0:T(1,128)S(1)}, s32[1,128]{1,0:T(1,128)S(1)}, u32[]{:S(2)}, u32[]{:S(2)}) collective-permute-start(s32[1,128]{1,0:T(1,128)S(1)} %get-tuple-element.24), channel_id=1, source_target_pairs={{0,2},{2,4},{4,6},{6,8},{8,10},{10,12},{12,14},{14,16},{16,18},{18... | collective-permute-start | bytes 1544 | tf_op jit(solution)/shard_map/ppermute | solution.py:15
  40.8 4.8 %collective-permute-start.5 = (s32[1,128]{1,0:T(1,128)S(1)}, s32[1,128]{1,0:T(1,128)S(1)}, u32[]{:S(2)}, u32[]{:S(2)}) collective-permute-start(s32[1,128]{1,0:T(1,128)S(1)} %get-tuple-element.25), channel_id=1, source_target_pairs={{0,6},{2,8},{4,10},{6,12},{8,14},{10,16},{12,18},{14,20},{16,22},{... | collective-permute-start | bytes 1544 | tf_op jit(solution)/shard_map/ppermute | solution.py:15
  40.9 6.3 %collective-permute-start.4 = (s32[1,128]{1,0:T(1,128)S(1)}, s32[1,128]{1,0:T(1,128)S(1)}, u32[]{:S(2)}, u32[]{:S(2)}) collective-permute-start(s32[1,128]{1,0:T(1,128)S(1)} %get-tuple-element.26), channel_id=1, source_target_pairs={{0,4},{2,6},{4,8},{6,10},{8,12},{10,14},{12,16},{14,18},{16,20},{1... | collective-permute-start | bytes 1544 | tf_op jit(solution)/shard_map/ppermute | solution.py:15
  121.7 8.9 %copy-start = (pred[512,512]{0,1:T(8,128)(4,1)S(1)}, pred[512,512]{0,1:T(8,128)(4,1)}, u32[]{:S(2)}) copy-start(pred[512,512]{0,1:T(8,128)(4,1)} %fusion.20) | copy-start | bytes 786436
  130.6 13.7 %copy-start.1 = (bf16[512,256]{0,1:T(8,128)(2,1)S(1)}, bf16[512,256]{0,1:T(8,128)(2,1)}, u32[]{:S(2)}) copy-start(bf16[512,256]{0,1:T(8,128)(2,1)} %copy.46) | copy-start | bytes 786436
Sparse Core Ops, SparseCore 0:
  38.4 51.8 all-gather.1
